TPU v7x, 256 devices: a whole 4x4x8 slice. The times are simulated.
256 devices in a mesh: bank: 32 (over z_hi, y, x), lane: 8 (over z_lo, core).
Axes of the slice: x: 4, y: 4, z: 8 (z_hi: 2, z_lo: 4; z = z_hi * 4 + z_lo), core: 2. Of those that a mesh axis runs over, the one named last changes fastest.
Arguments:
- amplitudes: float32 [2, 1024, 128, 128], P(None, ('bank', 'lane')), may hold values from -6 to 6
- energies: float32 [1024, 128, 128], P(('bank', 'lane')), may hold values from -2 to 2
- phase_angles: float32 [2, 128], replicated, may hold values from 0.3 to 1.2
- mix_angles: float32 [2, 4], replicated, may hold values from 0.3 to 1.2
Outputs:
- final_parts: float32 [2, 1024, 128, 128], P(None, ('bank', 'lane'))
- marginal: float32 [32, 128, 128], P('lane', 'bank')
All inputs are finite; a program needn't handle non-finite values.
Results may differ from a plain program's by a relative error of at most 0.0003.
Values sent between devices are 32-bit elements; how exact they have to be, the bound alone decides.
A program may use at most 64 MiB of HBM per device.

v0:
```python
import jax
import jax.numpy as jnp
from jax import lax
from jax.sharding import PartitionSpec as P

LAYERS = 2


def cut_along(value, dim, length):
    shape = value.shape
    parts = value.reshape(*shape[:dim], length, shape[dim] // length, *shape[dim + 1 :])
    return jnp.moveaxis(parts, dim, 0)


def sent_and_summed(value, axis, dim):
    length = lax.axis_size(axis)
    parts = lax.all_to_all(cut_along(value, dim, length), axis, 0, 0, tiled=True)
    return jnp.sum(parts, axis=0)


def count_bits(values, count):
    places = jnp.arange(count.bit_length() - 1, dtype=jnp.int32)
    return jnp.sum(values[..., None] >> places & 1, axis=-1)


def turn_table(count, angle):
    rank = jnp.arange(count, dtype=jnp.int32)
    apart = count_bits(rank[:, None] ^ rank[None, :], count)
    bits = count.bit_length() - 1
    size = jnp.cos(angle) ** (bits - apart).astype(jnp.float32) * jnp.sin(angle) ** apart.astype(
        jnp.float32
    )
    real_sign = jnp.where(apart % 4 == 0, 1.0, jnp.where(apart % 4 == 2, -1.0, 0.0)).astype(
        jnp.float32
    )
    imag_sign = jnp.where(apart % 4 == 1, -1.0, jnp.where(apart % 4 == 3, 1.0, 0.0)).astype(
        jnp.float32
    )
    return (size * real_sign, size * imag_sign)


def apply_along(values, dim, angle):
    real_part, imag_part = turn_table(values.shape[dim], angle)

    def times(table):
        moved = jnp.tensordot(values, table, axes=([dim], [0]), precision=lax.Precision.HIGHEST)
        return jnp.moveaxis(moved, -1, dim)

    by_real = times(real_part)
    by_imag = times(imag_part)
    return jnp.stack([by_real[0] - by_imag[1], by_real[1] + by_imag[0]])


def diagonal_step(values, levels, angle):
    turn = angle * levels
    return jnp.stack(
        [
            values[0] * jnp.cos(turn) + values[1] * jnp.sin(turn),
            values[1] * jnp.cos(turn) - values[0] * jnp.sin(turn),
        ]
    )


def on_device(amplitudes, energies, phase_angles, mix_angles):
    values = amplitudes
    for layer in range(LAYERS):
        values = diagonal_step(values, energies, phase_angles[layer])
        values = apply_along(values, 3, mix_angles[layer, 0])
        values = apply_along(values, 2, mix_angles[layer, 1])
        moved = lax.all_to_all(values, "bank", split_axis=2, concat_axis=1, tiled=True)
        moved = apply_along(moved, 1, mix_angles[layer, 2])
        values = lax.all_to_all(moved, "bank", split_axis=1, concat_axis=2, tiled=True)
        moved = lax.all_to_all(values, "lane", split_axis=3, concat_axis=1, tiled=True)
        spread = moved.reshape(2, lax.axis_size("lane"), -1, moved.shape[2], moved.shape[3])
        moved = apply_along(spread, 1, mix_angles[layer, 3]).reshape(moved.shape)
        values = lax.all_to_all(moved, "lane", split_axis=1, concat_axis=3, tiled=True)
    chance = values[0] * values[0] + values[1] * values[1]
    marginal = sent_and_summed(chance, "bank", 1) / lax.axis_size("bank")
    return (values, marginal)


def solution(mesh):
    placed = (P(None, ("bank", "lane"), None, None), P(("bank", "lane"), None, None), P(), P())
    return jax.shard_map(
        on_device,
        mesh=mesh,
        in_specs=placed,
        out_specs=(P(None, ("bank", "lane"), None, None), P("lane", "bank", None)),
        check_vma=False,
    )
```

profile of v0, /device:TPU:2, one launch (start us, length us, event | category | flops | bytes accessed | tf_op | source)
XLA Modules:
  0.0 225.9 jit_solution(11334041736106467783)
XLA Ops:
  0.6 1.7 fusion.220
  5.2 0.8 slice_bitcast_fusion
  6.0 2.1 fusion.14
  8.0 0.8 fusion.10
  8.8 0.8 fusion.11
  9.6 0.1 slice_subtract_fusion.7
  9.7 1.1 convolution_bitcast_fusion.10
  10.8 1.1 convolution_bitcast_fusion.11
  11.9 0.1 slice_subtract_fusion.6
  12.0 1.0 copy.91
  13.0 14.2 %all-to-all-start = ((f32[2,4,128,128]{3,1,0,2:T(4,128)}), f32[2,4,128,128]{3,1,0,2:T(4,128)S(1)}, u32[]{:S(2)}, u32[]{:S(2)}) async-start(f32[2,4,128,128]{3,1,0,2:T(4,128)} %copy.91), calls=%async_computation | async-start | bytes 1048576 | tf_op jit(solution)/shard_map/all_to_all | solution.py:70
  28.6 14.0 %all-to-all-done = f32[2,4,128,128]{3,1,0,2:T(4,128)S(1)} async-done(((f32[2,4,128,128]{3,1,0,2:T(4,128)}), f32[2,4,128,128]{3,1,0,2:T(4,128)S(1)}, u32[]{:S(2)}, u32[]{:S(2)}) %all-to-all-start) | async-done | bytes 524320 | tf_op jit(solution)/shard_map/all_to_all | solution.py:70
  42.7 0.1 copy.92
  42.8 0.3 copy.93
  43.1 1.1 convolution_bitcast_fusion.8
  44.2 1.1 convolution_bitcast_fusion.9
  45.3 0.1 slice_subtract_fusion.5
  45.5 0.3 copy.96
  45.7 18.1 %all_to_all.140 = f32[2,128,4,128]{3,2,0,1:T(4,128)S(1)} all-to-all(f32[2,128,4,128]{3,2,0,1:T(4,128)S(1)} %copy.96), channel_id=1, replica_groups=mesh['bank'=32,'lane'=8] {'bank'}, dimensions={1} | all-to-all | bytes 1048576 | tf_op jit(solution)/shard_map/all_to_all | solution.py:72
  63.8 0.1 copy.97
  63.9 0.3 copy.98
  64.3 1.0 copy.99
  65.3 9.1 %all-to-all-start.2 = ((f32[2,4,128,128]{2,1,0,3:T(4,128)}), f32[2,4,128,128]{2,1,0,3:T(4,128)S(1)}, u32[]{:S(2)}, u32[]{:S(2)}) async-start(f32[2,4,128,128]{2,1,0,3:T(4,128)} %copy.99), calls=%async_computation.2 | async-start | bytes 1048576 | tf_op jit(solution)/shard_map/all_to_all | solution.py:73
  75.6 14.0 %all-to-all-done.2 = f32[2,4,128,128]{2,1,0,3:T(4,128)S(1)} async-done(((f32[2,4,128,128]{2,1,0,3:T(4,128)}), f32[2,4,128,128]{2,1,0,3:T(4,128)S(1)}, u32[]{:S(2)}, u32[]{:S(2)}) %all-to-all-start.2) | async-done | bytes 524320 | tf_op jit(solution)/shard_map/all_to_all | solution.py:73
  89.7 0.9 convolution_bitcast_fusion.6
  90.6 0.9 convolution_bitcast_fusion.7
  91.4 0.1 slice_subtract_fusion.4
  91.7 0.9 copy.106
  92.5 3.5 %all-to-all-start.3 = ((f32[2,32,128,16]{2,3,0,1:T(8,128)}), f32[2,32,128,16]{2,3,0,1:T(8,128)S(1)}, u32[]{:S(2)}, u32[]{:S(2)}) async-start(f32[2,32,128,16]{2,3,0,1:T(8,128)} %copy.106), calls=%async_computation.3 | async-start | bytes 1048576 | tf_op jit(solution)/shard_map/all_to_all | solution.py:76
  99.1 12.2 %all-to-all-done.3 = f32[2,32,128,16]{2,3,0,1:T(8,128)S(1)} async-done(((f32[2,32,128,16]{2,3,0,1:T(8,128)}), f32[2,32,128,16]{2,3,0,1:T(8,128)S(1)}, u32[]{:S(2)}, u32[]{:S(2)}) %all-to-all-start.3) | async-done | bytes 524320 | tf_op jit(solution)/shard_map/all_to_all | solution.py:76
  111.4 0.1 copy.111
  111.6 0.1 copy.109
  111.7 1.0 add_bitcast_fusion
  112.7 0.8 fusion.8
  113.5 0.8 fusion.9
  114.3 0.1 slice_subtract_fusion.3
  114.4 1.1 convolution_bitcast_fusion.4
  115.5 1.1 convolution_bitcast_fusion.5
  116.6 0.1 slice_subtract_fusion.2
  116.7 1.0 copy.116
  117.7 5.3 %all-to-all-start.4 = ((f32[2,4,128,128]{3,1,0,2:T(4,128)}), f32[2,4,128,128]{3,1,0,2:T(4,128)S(1)}, u32[]{:S(2)}, u32[]{:S(2)}) async-start(f32[2,4,128,128]{3,1,0,2:T(4,128)} %copy.116), calls=%async_computation.4 | async-start | bytes 1048576 | tf_op jit(solution)/shard_map/all_to_all | solution.py:70
  124.3 15.7 %all-to-all-done.4 = f32[2,4,128,128]{3,1,0,2:T(4,128)S(1)} async-done(((f32[2,4,128,128]{3,1,0,2:T(4,128)}), f32[2,4,128,128]{3,1,0,2:T(4,128)S(1)}, u32[]{:S(2)}, u32[]{:S(2)}) %all-to-all-start.4) | async-done | bytes 524320 | tf_op jit(solution)/shard_map/all_to_all | solution.py:70
  140.0 0.1 copy.117
  140.1 0.3 copy.118
  140.5 1.1 convolution_bitcast_fusion.2
  141.6 1.1 convolution_bitcast_fusion.3
  142.8 0.3 copy.121
  143.1 20.4 %all_to_all.141 = f32[2,128,4,128]{3,2,0,1:T(4,128)S(1)} all-to-all(f32[2,128,4,128]{3,2,0,1:T(4,128)S(1)} %copy.121), channel_id=1, replica_groups=mesh['bank'=32,'lane'=8] {'bank'}, dimensions={1} | all-to-all | bytes 1048576 | tf_op jit(solution)/shard_map/all_to_all | solution.py:72
  163.5 0.1 copy.122
  163.6 0.3 copy.123
  163.9 1.0 copy.124
  164.9 3.5 %all-to-all-start.6 = ((f32[2,4,128,128]{2,1,0,3:T(4,128)}), f32[2,4,128,128]{2,1,0,3:T(4,128)S(1)}, u32[]{:S(2)}, u32[]{:S(2)}) async-start(f32[2,4,128,128]{2,1,0,3:T(4,128)} %copy.124), calls=%async_computation.6 | async-start | bytes 1048576 | tf_op jit(solution)/shard_map/all_to_all | solution.py:73
  169.9 13.8 %all-to-all-done.6 = f32[2,4,128,128]{2,1,0,3:T(4,128)S(1)} async-done(((f32[2,4,128,128]{2,1,0,3:T(4,128)}), f32[2,4,128,128]{2,1,0,3:T(4,128)S(1)}, u32[]{:S(2)}, u32[]{:S(2)}) %all-to-all-start.6) | async-done | bytes 524320 | tf_op jit(solution)/shard_map/all_to_all | solution.py:73
  183.7 0.9 convolution_bitcast_fusion
  184.6 0.9 convolution_bitcast_fusion.1
  185.8 17.7 %all_to_all.142 = f32[2,32,128,16]{2,3,0,1:T(8,128)S(1)} all-to-all(f32[2,32,128,16]{2,3,0,1:T(8,128)S(1)} %copy.131), channel_id=1, replica_groups=mesh['bank'=32,'lane'=8] {'lane'}, dimensions={1} | all-to-all | bytes 1048576 | tf_op jit(solution)/shard_map/all_to_all | solution.py:76
  203.6 0.7 copy.134
  204.3 0.6 add.130
  204.9 0.7 copy.135
  205.7 8.0 %all-to-all-start.8 = ((f32[32,4,4,128]{3,2,1,0:T(4,128)}), f32[32,4,4,128]{3,2,1,0:T(4,128)S(1)}, u32[]{:S(2)}, u32[]{:S(2)}) async-start(f32[32,4,4,128]{3,2,1,0:T(4,128)} %copy.135), calls=%async_computation.8 | async-start | bytes 524288 | tf_op jit(solution)/shard_map/all_to_all | solution.py:17
  213.7 1.0 copy.136
  214.7 10.5 %all-to-all-done.8 = f32[32,4,4,128]{3,2,1,0:T(4,128)S(1)} async-done(((f32[32,4,4,128]{3,2,1,0:T(4,128)}), f32[32,4,4,128]{3,2,1,0:T(4,128)S(1)}, u32[]{:S(2)}, u32[]{:S(2)}) %all-to-all-start.8) | async-done | bytes 262176 | tf_op jit(solution)/shard_map/all_to_all | solution.py:17
  225.2 0.1 reduce_sum.29
  225.3 0.6 broadcast_multiply_fusion
  (26 shorter events, 0.9 us)
Async XLA Ops:
  13.0 29.7 %all-to-all-start = ((f32[2,4,128,128]{3,1,0,2:T(4,128)}), f32[2,4,128,128]{3,1,0,2:T(4,128)S(1)}, u32[]{:S(2)}, u32[]{:S(2)}) async-start(f32[2,4,128,128]{3,1,0,2:T(4,128)} %copy.91), calls=%async_computation | async-start | bytes 1048576 | tf_op jit(solution)/shard_map/all_to_all | solution.py:70
  65.3 24.4 %all-to-all-start.2 = ((f32[2,4,128,128]{2,1,0,3:T(4,128)}), f32[2,4,128,128]{2,1,0,3:T(4,128)S(1)}, u32[]{:S(2)}, u32[]{:S(2)}) async-start(f32[2,4,128,128]{2,1,0,3:T(4,128)} %copy.99), calls=%async_computation.2 | async-start | bytes 1048576 | tf_op jit(solution)/shard_map/all_to_all | solution.py:73
  92.5 18.8 %all-to-all-start.3 = ((f32[2,32,128,16]{2,3,0,1:T(8,128)}), f32[2,32,128,16]{2,3,0,1:T(8,128)S(1)}, u32[]{:S(2)}, u32[]{:S(2)}) async-start(f32[2,32,128,16]{2,3,0,1:T(8,128)} %copy.106), calls=%async_computation.3 | async-start | bytes 1048576 | tf_op jit(solution)/shard_map/all_to_all | solution.py:76
  99.1 12.6 %copy-start = (f32[4,128,128]{2,1,0:T(8,128)S(1)}, f32[4,128,128]{2,1,0:T(8,128)}, u32[]{:S(2)}) copy-start(f32[4,128,128]{2,1,0:T(8,128)} %param.5) | copy-start | bytes 786436
  117.7 22.3 %all-to-all-start.4 = ((f32[2,4,128,128]{3,1,0,2:T(4,128)}), f32[2,4,128,128]{3,1,0,2:T(4,128)S(1)}, u32[]{:S(2)}, u32[]{:S(2)}) async-start(f32[2,4,128,128]{3,1,0,2:T(4,128)} %copy.116), calls=%async_computation.4 | async-start | bytes 1048576 | tf_op jit(solution)/shard_map/all_to_all | solution.py:70
  164.9 18.8 %all-to-all-start.6 = ((f32[2,4,128,128]{2,1,0,3:T(4,128)}), f32[2,4,128,128]{2,1,0,3:T(4,128)S(1)}, u32[]{:S(2)}, u32[]{:S(2)}) async-start(f32[2,4,128,128]{2,1,0,3:T(4,128)} %copy.124), calls=%async_computation.6 | async-start | bytes 1048576 | tf_op jit(solution)/shard_map/all_to_all | solution.py:73
  205.7 19.5 %all-to-all-start.8 = ((f32[32,4,4,128]{3,2,1,0:T(4,128)}), f32[32,4,4,128]{3,2,1,0:T(4,128)S(1)}, u32[]{:S(2)}, u32[]{:S(2)}) async-start(f32[32,4,4,128]{3,2,1,0:T(4,128)} %copy.135), calls=%async_computation.8 | async-start | bytes 524288 | tf_op jit(solution)/shard_map/all_to_all | solution.py:17
where the time goes:
time: 228 us; the launch traced here: 226 us
  waiting for transfers between devices  80.3 us (35%)
  blocking collectives  56.3 us (25%)
  starting transfers between devices  43.6 us (19%)
  matrix products  15.4 us (7%)
  local copies, waits for them, and re-layouts  13.3 us (6%)
  between operations  12.4 us (5%)
  other arithmetic  4.54 us (2%)
    all_to_all x2, blocking collectives, on_device(): lax.all_to_all(moved, 'bank', split_axis=1, concat_axis=2, tiled=True)  38.5 us
    all_to_all x2, waiting for transfers between devices, on_device(): lax.all_to_all(values, 'bank', split_axis=2, concat_axis=1, tiled=True)  29.8 us
    all_to_all x2, waiting for transfers between devices, on_device(): lax.all_to_all(values, 'lane', split_axis=3, concat_axis=1, tiled=True)  27.8 us
    all_to_all x2, starting transfers between devices, on_device(): lax.all_to_all(values, 'bank', split_axis=2, concat_axis=1, tiled=True)  19.6 us
    all_to_all x1, blocking collectives, on_device(): lax.all_to_all(moved, 'lane', split_axis=1, concat_axis=3, tiled=True)  17.7 us
    dot_general x16, matrix products, times(): jnp.tensordot(values, table, axes=([dim], [0]), precision=lax.Precision.H...  15.4 us
    all_to_all x2, starting transfers between devices, on_device(): lax.all_to_all(values, 'lane', split_axis=3, concat_axis=1, tiled=True)  12.6 us
    all_to_all x1, waiting for transfers between devices, on_device(): lax.all_to_all(moved, 'lane', split_axis=1, concat_axis=3, tiled=True)  12.2 us
  transfers between devices with their start and end apart: 6, of which 6 were waited for; matrix products, arithmetic and copies ran while one was open for 0% of the time, Pallas kernels for 0%

commit v1 on v0

v1 whole, which is shorter than its diff:
```python
import functools

import jax
import jax.numpy as jnp
from jax import lax
from jax.experimental import pallas as pl
from jax.experimental.pallas import tpu as pltpu
from jax.sharding import PartitionSpec as P

MESH = pl.DeviceIdType.MESH
F32 = jnp.float32
BF16 = jnp.bfloat16

Z_STEPS = (4, 3, 5, 2, 6, 1, 7)
XY_STEPS = tuple((dx, dy) for dx in (2, 1, 3, 0) for dy in (2, 1, 3, 0) if dx or dy)
STAGES = 20


def sine_cosine(angle):
    half = 0.5 * angle
    w = half * half
    s = jnp.full_like(w, -1.0 / 39916800.0)
    for term in (1.0 / 362880.0, -1.0 / 5040.0, 1.0 / 120.0, -1.0 / 6.0, 1.0):
        s = s * w + term
    s = s * half
    c = jnp.full_like(w, 1.0 / 479001600.0)
    for term in (-1.0 / 3628800.0, 1.0 / 40320.0, -1.0 / 720.0, 1.0 / 24.0, -0.5, 1.0):
        c = c * w + term
    return 2.0 * s * c, 1.0 - 2.0 * s * s


def split(value):
    high = value.astype(BF16)
    return high, (value - high.astype(F32)).astype(BF16)


def times(left, right):
    (lh, ll), (rh, rl) = left, right
    dot = functools.partial(jnp.dot, preferred_element_type=F32)
    return dot(lh, rh) + dot(lh, rl) + dot(ll, rh)


def kernel(amps, energies, phases, mixes, out, marg, *scratch):
    (tables, canon, moved, other, e_send, e_mid, e_got, s_buf, s_mid, s_got, t_buf, t_mid, t_oth, t_mix, t_got,
     held, p_send, p_got, p_sum, p_far, send_sem, recv_sem) = scratch
    bank, lane = lax.axis_index("bank"), lax.axis_index("lane")
    x, y, z_hi = bank % 4, (bank // 4) % 4, bank // 16
    z, core = z_hi * 4 + lane // 2, lane % 2
    xy = y * 4 + x

    def z_peer(step):
        there = (z + step) % 8
        return there, ((there // 4) * 16 + xy, (there % 4) * 2 + core)

    def xy_peer(step):
        there = ((y + step[1]) % 4) * 4 + (x + step[0]) % 4
        return there, (z_hi * 16 + there, lane)

    partner = (bank, (lane // 2) * 2 + 1 - core)
    z_peers = [z_peer(step) for step in Z_STEPS]
    xy_peers = [xy_peer(step) for step in XY_STEPS]

    def remote(src, dst, stage, device):
        return pltpu.make_async_remote_copy(
            src_ref=src, dst_ref=dst, send_sem=send_sem.at[stage], recv_sem=recv_sem.at[stage],
            device_id=device, device_id_type=MESH,
        )

    def send_z(src, dst, stage):
        for there, device in z_peers:
            remote(src.at[there], dst.at[z], stage, device).start()
        dst[z] = src[z]

    def send_xy(src, dst, stage, unit):
        for there, device in xy_peers:
            remote(
                src.at[:, pl.ds(pl.multiple_of(there * unit, unit), unit), :],
                dst.at[:, pl.ds(pl.multiple_of(xy * unit, unit), unit), :],
                stage, device,
            ).start()
        own = pl.ds(pl.multiple_of(xy * unit, unit), unit)
        dst[:, own, :] = src[:, own, :]

    def all_of(ref, sem):
        return pltpu.make_async_copy(ref, ref, sem)

    def z_bytes(buf):
        return buf.at[pl.ds(0, 7)]

    def xy_bytes(buf, unit):
        return buf.at[:, pl.ds(0, 15 * unit), :]

    barrier = pltpu.get_barrier_semaphore()
    for _, device in z_peers + xy_peers:
        pl.semaphore_signal(barrier, inc=1, device_id=device, device_id_type=MESH)
    pl.semaphore_signal(barrier, inc=1, device_id=partner, device_id_type=MESH)

    for r0 in range(2):
        for sz in range(8):
            for r1 in range(2):
                e_send[r0, sz, pl.ds(r1, 16, stride=2), :] = energies[
                    sz // 2, pl.ds((sz % 2) * 64 + 2 * r1 + r0, 16, stride=4), :
                ]
    pl.semaphore_wait(barrier, 23)
    send_z(e_send.at[0], e_mid.at[0], 0)
    send_xy(e_send.at[1], e_mid.at[1], 1, 2)

    mix_sin, mix_cos = sine_cosine(mixes[...])

    def cs(layer, group, shape):
        at = (slice(layer, layer + 1), slice(group, group + 1))
        return jnp.broadcast_to(mix_cos[at], shape), jnp.broadcast_to(mix_sin[at], shape)

    row = lax.broadcasted_iota(jnp.int32, (128, 128), 0)
    column = lax.broadcasted_iota(jnp.int32, (128, 128), 1)
    apart = row ^ column

    def build(slot, layer, groups, on_left):
        size, count = None, None
        for k, group in enumerate(groups):
            c, s = cs(layer, group, (128, 128))
            bit = (apart >> k) & 1
            factor = jnp.where(bit == 1, s, c)
            size = factor if size is None else size * factor
            count = bit if count is None else count + bit
        odd = (count & 1) == 1
        sign = 1.0 - (count & 2).astype(F32)
        re = jnp.where(odd, 0.0, size * sign)
        im = jnp.where(odd, -size * sign, 0.0)
        for half, (real, imag) in enumerate(zip(split(re), split(im))):
            tables[slot, half, 0:128, 0:128] = real
            tables[slot, half, 128:256, 128:256] = real
            tables[slot, half, 0:128, 128:256] = -imag if on_left else imag
            tables[slot, half, 128:256, 0:128] = imag if on_left else -imag

    def table(slot):
        return tables[slot, 0], tables[slot, 1]

    lanes = (0,) * 7
    rows = (1,) * 5 + (2, 2)
    chips = (2,) * 4 + (3, 3) + (2,)
    build(0, 0, lanes, False)
    build(1, 0, rows, True)

    def turned(re, im, levels, layer):
        angle = jnp.broadcast_to(phases[layer:layer + 1, :], levels.shape) * levels
        s, c = sine_cosine(angle)
        return re * c + im * s, im * c - re * s

    def mixed(u, v, c, s):
        (ur, ui), (vr, vi) = u, v
        return (c * ur + s * vi, c * ui - s * vr), (c * vr + s * ui, c * vi - s * ur)

    shape = (32, 128)
    c1, s1 = cs(0, 1, shape)
    for t in range(4):
        parts = {}
        for q in range(4):
            at = pl.ds(q, 32, stride=4)
            parts[q] = turned(amps[0, t, at, :], amps[1, t, at, :], energies[t, at, :], 0)
        for low, high in ((0, 1), (2, 3), (0, 2), (1, 3)):
            parts[low], parts[high] = mixed(parts[low], parts[high], c1, s1)
        for q in range(4):
            place = ((q % 2) * 2 + q // 2) * 128 + t * 32
            canon[place:place + 32, 0:128] = parts[q][0]
            canon[place:place + 32, 128:256] = parts[q][1]
    for r0 in range(2):
        done = times(split(canon[r0 * 256:r0 * 256 + 256, :]), table(0))
        for r1 in range(2):
            for part in range(2):
                moved[r0, part * 128:part * 128 + 128, r1 * 128:r1 * 128 + 128] = done[
                    r1 * 128:r1 * 128 + 128, part * 128:part * 128 + 128
                ]
        remote(moved.at[r0], other.at[r0], 2 + r0, partner).start()

    def spread(buf, r0, value):
        for sz in range(8):
            for part in range(2):
                for r1 in range(2):
                    buf[r0, sz, pl.ds(2 * part + r1, 16, stride=4), :] = value[
                        part * 128 + sz * 16:part * 128 + sz * 16 + 16, r1 * 128:r1 * 128 + 128
                    ]

    def gathered(buf, r0):
        columns = []
        for r1 in range(2):
            columns.append(jnp.concatenate(
                [buf[r0, sz, pl.ds(2 * part + r1, 16, stride=4), :] for part in range(2) for sz in range(8)], axis=0
            ))
        return jnp.concatenate(columns, axis=1)

    c3, s3 = cs(0, 3, (128, 256))
    for r0 in range(2):
        all_of(other.at[r0], recv_sem.at[2 + r0]).wait()
        re = c3 * moved[r0, 0:128, :] + s3 * other[r0, 128:256, :]
        im = c3 * moved[r0, 128:256, :] - s3 * other[r0, 0:128, :]
        spread(s_buf, r0, times(table(1), split(jnp.concatenate([re, im], axis=0))))
        if r0 == 0:
            send_z(s_buf.at[0], s_mid.at[0], 4)
        else:
            send_xy(s_buf.at[1], s_mid.at[1], 5, 4)

    all_of(z_bytes(e_mid.at[0]), recv_sem.at[0]).wait()
    send_xy(e_mid.at[0], e_got.at[0], 6, 2)
    all_of(xy_bytes(e_mid.at[1], 2), recv_sem.at[1]).wait()
    send_z(e_mid.at[1], e_got.at[1], 7)

    all_of(xy_bytes(s_mid.at[1], 4), recv_sem.at[5]).wait()
    send_z(s_mid.at[1], s_got.at[1], 8)
    build(2, 0, chips, True)
    build(3, 1, chips, True)
    all_of(z_bytes(s_mid.at[0]), recv_sem.at[4]).wait()
    send_xy(s_mid.at[0], s_got.at[0], 9, 4)
    build(4, 1, lanes, False)
    build(5, 1, rows, True)

    def middle(r0):
        value = times(table(2), split(gathered(s_got, r0)))
        c, s = cs(1, 1, (128, 128))
        parts = []
        for r1 in range(2):
            levels = jnp.concatenate([e_got[r0, sz, pl.ds(r1, 16, stride=2), :] for sz in range(8)], axis=0)
            at = slice(r1 * 128, r1 * 128 + 128)
            parts.append(turned(value[0:128, at], value[128:256, at], levels, 1))
        parts = mixed(parts[0], parts[1], c, s)
        value = jnp.concatenate([jnp.concatenate(part, axis=1) for part in parts], axis=0)
        value = times(split(value), table(4))
        value = jnp.concatenate(
            [jnp.concatenate([value[0:128, at], value[128:256, at]], axis=1) for at in (slice(0, 128), slice(128, 256))],
            axis=0,
        )
        held[r0] = times(table(3), split(value))

    all_of(xy_bytes(e_got.at[0], 2), recv_sem.at[6]).wait()
    all_of(xy_bytes(s_got.at[0], 4), recv_sem.at[9]).wait()
    middle(0)
    all_of(z_bytes(e_got.at[1]), recv_sem.at[7]).wait()
    all_of(z_bytes(s_got.at[1]), recv_sem.at[8]).wait()
    middle(1)

    c0, s0 = cs(1, 1, (128, 256))
    first, second = mixed(
        (held[0, 0:128, :], held[0, 128:256, :]), (held[1, 0:128, :], held[1, 128:256, :]), c0, s0
    )
    spread(t_buf, 1, jnp.concatenate(second, axis=0))
    send_z(t_buf.at[1], t_mid.at[1], 10)
    spread(t_buf, 0, jnp.concatenate(first, axis=0))
    send_xy(t_buf.at[0], t_mid.at[0], 11, 4)

    ck, sk = cs(1, 3, (16, 128))

    def core_mixed(r0):
        for sz in range(8):
            for part in range(2):
                for r1 in range(2):
                    own = t_mid[r0, sz, pl.ds(2 * part + r1, 16, stride=4), :]
                    far = t_oth[r0, sz, pl.ds(2 * (1 - part) + r1, 16, stride=4), :]
                    t_mix[r0, sz, pl.ds(2 * part + r1, 16, stride=4), :] = (
                        ck * own + sk * far if part == 0 else ck * own - sk * far
                    )

    all_of(xy_bytes(t_mid.at[0], 4), recv_sem.at[11]).wait()
    remote(t_mid.at[0], t_oth.at[0], 12, partner).start()
    all_of(t_oth.at[0], recv_sem.at[12]).wait()
    core_mixed(0)
    send_z(t_mix.at[0], t_got.at[0], 13)
    all_of(z_bytes(t_mid.at[1]), recv_sem.at[10]).wait()
    remote(t_mid.at[1], t_oth.at[1], 14, partner).start()
    all_of(t_oth.at[1], recv_sem.at[14]).wait()
    core_mixed(1)
    send_xy(t_mix.at[1], t_got.at[1], 15, 4)

    def final(r0):
        value = times(table(5), split(gathered(t_got, r0)))
        for part in range(2):
            for t in range(4):
                for r1 in range(2):
                    out[part, t, pl.ds(2 * r1 + r0, 32, stride=4), :] = value[
                        part * 128 + t * 32:part * 128 + t * 32 + 32, r1 * 128:r1 * 128 + 128
                    ]
        chance = value[0:128, :] * value[0:128, :] + value[128:256, :] * value[128:256, :]
        for t in range(4):
            for r6 in range(2):
                for r1 in range(2):
                    at = t * 32 + r6 * 16
                    p_send[r6, pl.ds(t * 4 + r1 * 2 + r0, 16, stride=16), :] = chance[
                        at:at + 16, r1 * 128:r1 * 128 + 128
                    ]

    all_of(xy_bytes(t_got.at[1], 4), recv_sem.at[15]).wait()
    final(1)
    all_of(z_bytes(t_got.at[0]), recv_sem.at[13]).wait()
    final(0)

    for there, device in xy_peers:
        remote(
            p_send.at[:, pl.ds(pl.multiple_of(there * 16, 16), 16), :], p_got.at[xy], 16, device
        ).start()
    p_got[xy] = p_send[:, pl.ds(pl.multiple_of(xy * 16, 16), 16), :]
    all_of(p_got.at[pl.ds(0, 15)], recv_sem.at[16]).wait()
    total = p_got[0]
    for k in range(1, 16):
        total = total + p_got[k]
    p_sum[...] = total
    far = remote(p_sum.at[1 - z_hi], p_far, 17, ((1 - z_hi) * 16 + xy, lane))
    far.start()
    all_of(p_far, recv_sem.at[17]).wait()
    whole = (p_sum[z_hi] + p_far[...]) * (1.0 / 32.0)
    for t in range(4):
        marg[t] = whole[t * 4:t * 4 + 4, :]

    for stage, buf in (
        (0, z_bytes(e_send.at[0])), (7, z_bytes(e_mid.at[1])), (4, z_bytes(s_buf.at[0])), (8, z_bytes(s_mid.at[1])),
        (10, z_bytes(t_buf.at[1])), (13, z_bytes(t_mix.at[0])),
        (1, xy_bytes(e_send.at[1], 2)), (6, xy_bytes(e_mid.at[0], 2)),
        (5, xy_bytes(s_buf.at[1], 4)), (9, xy_bytes(s_mid.at[0], 4)), (11, xy_bytes(t_buf.at[0], 4)),
        (15, xy_bytes(t_mix.at[1], 4)),
        (2, moved.at[0]), (3, moved.at[1]), (12, t_mid.at[0]), (14, t_mid.at[1]),
        (16, p_got.at[pl.ds(0, 15)]), (17, p_far),
    ):
        all_of(buf, send_sem.at[stage]).wait()


def on_device(amplitudes, energies, phase_angles, mix_angles):
    vmem = pl.BlockSpec(memory_space=pltpu.VMEM)
    half = pltpu.VMEM((2, 8, 64, 128), F32)
    levels = pltpu.VMEM((2, 8, 32, 128), F32)
    wide = pltpu.VMEM((2, 256, 256), F32)
    return pl.pallas_call(
        kernel,
        out_shape=(
            jax.ShapeDtypeStruct((2, 4, 128, 128), F32),
            jax.ShapeDtypeStruct((4, 4, 128), F32),
        ),
        in_specs=[vmem] * 4,
        out_specs=(vmem, vmem),
        scratch_shapes=[
            pltpu.VMEM((6, 2, 256, 256), BF16),
            pltpu.VMEM((512, 256), F32),
            wide, wide,
            levels, levels, levels,
            half, half, half,
            half, half, half, half, half,
            wide,
            pltpu.VMEM((2, 256, 128), F32),
            pltpu.VMEM((16, 2, 16, 128), F32),
            pltpu.VMEM((2, 16, 128), F32),
            pltpu.VMEM((16, 128), F32),
            pltpu.SemaphoreType.DMA((STAGES,)),
            pltpu.SemaphoreType.DMA((STAGES,)),
        ],
        compiler_params=pltpu.CompilerParams(
            collective_id=0, has_side_effects=True, vmem_limit_bytes=48 * 1024 * 1024
        ),
    )(amplitudes, energies, phase_angles, mix_angles)


def solution(mesh):
    placed = (P(None, ("bank", "lane"), None, None), P(("bank", "lane"), None, None), P(), P())
    return jax.shard_map(
        on_device,
        mesh=mesh,
        in_specs=placed,
        out_specs=(P(None, ("bank", "lane"), None, None), P("lane", "bank", None)),
        check_vma=False,
    )
```

time: 228 us -> 61.8 us (0.27)
  waiting for transfers between devices: 80.3 us -> 0 us
  blocking collectives: 56.3 us -> 0 us
  Pallas kernels: 0 us -> 55.9 us
  starting transfers between devices: 43.6 us -> 0 us
  matrix products: 15.4 us -> 0 us
  between operations: 12.4 us -> 0.65 us
  local copies, waits for them, and re-layouts: 13.3 us -> 4.73 us
  other arithmetic: 4.54 us -> 0 us
    all_to_all x6 -> x0, waiting for transfers between devices: 80.3 us -> none  [the longest x2 29.8 us: on_device(): lax.all_to_all(values, 'bank', split_axis=2, concat_axis=1, tiled=True)]
    all_to_all x3 -> x0, blocking collectives: 56.3 us -> none  [the longest x2 38.5 us: on_device(): lax.all_to_all(moved, 'bank', split_axis=1, concat_axis=2, tiled=True)]
    pallas_call x0 -> x1, Pallas kernels: none -> 55.9 us  [on_device(): pl.pallas_call(kernel, out_shape=(jax.ShapeDtypeStruct((2, 4, 128, 128),...]
    all_to_all x6 -> x0, starting transfers between devices: 43.6 us -> none  [the longest x2 19.6 us: on_device(): lax.all_to_all(values, 'bank', split_axis=2, concat_axis=1, tiled=True)]
    dot_general x16 -> x0, matrix products: 15.4 us -> none  [times(): jnp.tensordot(values, table, axes=([dim], [0]), precision=lax.Precision.H...]
    all_to_all x13 -> x0, local copies, waits for them, and re-layouts: 3.87 us -> none  [the longest x6 2.88 us: on_device(): lax.all_to_all(moved, 'bank', split_axis=1, concat_axis=2, tiled=True)]
    unnamed x3 -> x10, local copies, waits for them, and re-layouts: 1 us -> 4.73 us
    another operation x6 -> x0, local copies, waits for them, and re-layouts: 3.42 us -> none  [apply_along(): return jnp.stack([by_real[0] - by_imag[1], by_real[1] + by_imag[0]])]
  transfers between devices with their start and end apart: 6 -> 0, of which waited for: 6 -> 0; matrix products, arithmetic and copies ran while one was open for 0% -> 0% of each run, Pallas kernels for 0% -> 0%
where the time goes in v1:
time: 61.8 us; the launch traced here: 61.3 us
  Pallas kernels  55.9 us (90%)
  local copies, waits for them, and re-layouts  4.73 us (8%)
  between operations  0.65 us (1%)
    pallas_call x1, Pallas kernels, on_device(): pl.pallas_call(kernel, out_shape=(jax.ShapeDtypeStruct((2, 4, 128, 128),...  55.9 us
    unnamed x10, local copies, waits for them, and re-layouts  4.73 us

profile of v1, /device:TPU:2, one launch (start us, length us, event | category | flops | bytes accessed | tf_op | source)
XLA Modules:
  0.0 61.3 jit_solution(2977458189851268454)
XLA Ops:
  0.6 0.0 copy-start
  0.6 1.0 %copy-done = f32[2,4,128,128]{3,2,1,0:T(8,128)S(1)} copy-done((f32[2,4,128,128]{3,2,1,0:T(8,128)S(1)}, f32[2,4,128,128]{3,2,1,0:T(8,128)}, u32[]{:S(2)}) %copy-start) | copy-done | bytes 524312
  1.7 0.0 copy-start.1
  1.7 0.9 %copy-done.1 = f32[4,128,128]{2,1,0:T(8,128)S(1)} copy-done((f32[4,128,128]{2,1,0:T(8,128)S(1)}, f32[4,128,128]{2,1,0:T(8,128)}, u32[]{:S(2)}) %copy-start.1) | copy-done | bytes 262168
  2.6 0.0 copy-start.2
  2.6 0.7 %copy-done.2 = f32[2,128]{1,0:T(2,128)S(1)} copy-done((f32[2,128]{1,0:T(2,128)S(1)}, f32[2,128]{1,0:T(2,128)}, u32[]{:S(2)}) %copy-start.2) | copy-done | bytes 1048
  3.3 0.0 copy-start.3
  3.3 0.7 %copy-done.3 = f32[2,4]{1,0:T(2,128)S(1)} copy-done((f32[2,4]{1,0:T(2,128)S(1)}, f32[2,4]{1,0:T(2,128)}, u32[]{:S(2)}) %copy-start.3) | copy-done | bytes 56
  4.0 55.9 %shard_map.59 = (f32[2,4,128,128]{3,2,1,0:T(8,128)S(1)}, f32[4,4,128]{2,1,0:T(4,128)S(1)}) custom-call(f32[2,4,128,128]{3,2,1,0:T(8,128)S(1)} %copy-done, f32[4,128,128]{2,1,0:T(8,128)S(1)} %copy-done.1, f32[2,128]{1,0:T(2,128)S(1)} %copy-done.2, f32[2,4]{1,0:T(2,128)S(1)} %copy-done.3), custom_call_target="tpu_custom_call" | custom-call | tf_op jit(solution)/shard_map/pallas_call | solution.py:329
  59.9 0.8 %copy.8 = f32[2,4,128,128]{3,2,1,0:T(8,128)} copy(f32[2,4,128,128]{3,2,1,0:T(8,128)S(1)} %get-tuple-element.4) | data formatting | bytes 1048576
  60.7 0.6 copy.9
Async XLA Ops:
  0.6 1.0 %copy-start = (f32[2,4,128,128]{3,2,1,0:T(8,128)S(1)}, f32[2,4,128,128]{3,2,1,0:T(8,128)}, u32[]{:S(2)}) copy-start(f32[2,4,128,128]{3,2,1,0:T(8,128)} %amps.1) | copy-start | bytes 1572868
  1.7 0.9 %copy-start.1 = (f32[4,128,128]{2,1,0:T(8,128)S(1)}, f32[4,128,128]{2,1,0:T(8,128)}, u32[]{:S(2)}) copy-start(f32[4,128,128]{2,1,0:T(8,128)} %energies.1) | copy-start | bytes 786436
  2.6 0.7 %copy-start.2 = (f32[2,128]{1,0:T(2,128)S(1)}, f32[2,128]{1,0:T(2,128)}, u32[]{:S(2)}) copy-start(f32[2,128]{1,0:T(2,128)} %phases.1) | copy-start | bytes 3076
  3.3 0.7 %copy-start.3 = (f32[2,4]{1,0:T(2,128)S(1)}, f32[2,4]{1,0:T(2,128)}, u32[]{:S(2)}) copy-start(f32[2,4]{1,0:T(2,128)} %mixes.1) | copy-start | bytes 100

commit v2 on v1

--- a/solution.py
+++ b/solution.py
@@ -40,8 +40,8 @@
     return dot(lh, rh) + dot(lh, rl) + dot(ll, rh)
 
 
-def kernel(amps, energies, phases, mixes, out, marg, *scratch):
-    (tables, canon, moved, other, e_send, e_mid, e_got, s_buf, s_mid, s_got, t_buf, t_mid, t_oth, t_mix, t_got,
+def kernel(amps_in, energies_in, phases_in, mixes_in, out, marg, *scratch):
+    (amps, energies, phases, mixes, in_sem, tables, canon, moved, other, e_send, e_mid, e_got, s_buf, s_mid, s_got, t_buf, t_mid, t_oth, t_mix, t_got,
      held, p_send, p_got, p_sum, p_far, send_sem, recv_sem) = scratch
     bank, lane = lax.axis_index("bank"), lax.axis_index("lane")
     x, y, z_hi = bank % 4, (bank // 4) % 4, bank // 16
@@ -95,16 +95,28 @@
         pl.semaphore_signal(barrier, inc=1, device_id=device, device_id_type=MESH)
     pl.semaphore_signal(barrier, inc=1, device_id=partner, device_id_type=MESH)
 
+    loads = [
+        pltpu.make_async_copy(src, dst, in_sem.at[k])
+        for k, (src, dst) in enumerate(
+            ((energies_in, energies), (mixes_in, mixes), (phases_in, phases), (amps_in, amps))
+        )
+    ]
+    for load in loads:
+        load.start()
+    loads[0].wait()
     for r0 in range(2):
         for sz in range(8):
             for r1 in range(2):
                 e_send[r0, sz, pl.ds(r1, 16, stride=2), :] = energies[
                     sz // 2, pl.ds((sz % 2) * 64 + 2 * r1 + r0, 16, stride=4), :
                 ]
-    pl.semaphore_wait(barrier, 23)
+    with jax.named_scope("barrier"):
+        pl.semaphore_wait(barrier, 23)
     send_z(e_send.at[0], e_mid.at[0], 0)
     send_xy(e_send.at[1], e_mid.at[1], 1, 2)
 
+    for load in loads[1:]:
+        load.wait()
     mix_sin, mix_cos = sine_cosine(mixes[...])
 
     def cs(layer, group, shape):
@@ -191,7 +203,8 @@
 
     c3, s3 = cs(0, 3, (128, 256))
     for r0 in range(2):
-        all_of(other.at[r0], recv_sem.at[2 + r0]).wait()
+        with jax.named_scope("w" + str(2 + r0)):
+            all_of(other.at[r0], recv_sem.at[2 + r0]).wait()
         re = c3 * moved[r0, 0:128, :] + s3 * other[r0, 128:256, :]
         im = c3 * moved[r0, 128:256, :] - s3 * other[r0, 0:128, :]
         spread(s_buf, r0, times(table(1), split(jnp.concatenate([re, im], axis=0))))
@@ -200,16 +213,20 @@
         else:
             send_xy(s_buf.at[1], s_mid.at[1], 5, 4)
 
-    all_of(z_bytes(e_mid.at[0]), recv_sem.at[0]).wait()
+    with jax.named_scope("w" + str(0)):
+        all_of(z_bytes(e_mid.at[0]), recv_sem.at[0]).wait()
     send_xy(e_mid.at[0], e_got.at[0], 6, 2)
-    all_of(xy_bytes(e_mid.at[1], 2), recv_sem.at[1]).wait()
+    with jax.named_scope("w" + str(1)):
+        all_of(xy_bytes(e_mid.at[1], 2), recv_sem.at[1]).wait()
     send_z(e_mid.at[1], e_got.at[1], 7)
 
-    all_of(xy_bytes(s_mid.at[1], 4), recv_sem.at[5]).wait()
+    with jax.named_scope("w" + str(5)):
+        all_of(xy_bytes(s_mid.at[1], 4), recv_sem.at[5]).wait()
     send_z(s_mid.at[1], s_got.at[1], 8)
     build(2, 0, chips, True)
     build(3, 1, chips, True)
-    all_of(z_bytes(s_mid.at[0]), recv_sem.at[4]).wait()
+    with jax.named_scope("w" + str(4)):
+        all_of(z_bytes(s_mid.at[0]), recv_sem.at[4]).wait()
     send_xy(s_mid.at[0], s_got.at[0], 9, 4)
     build(4, 1, lanes, False)
     build(5, 1, rows, True)
@@ -231,11 +248,15 @@
         )
         held[r0] = times(table(3), split(value))
 
-    all_of(xy_bytes(e_got.at[0], 2), recv_sem.at[6]).wait()
-    all_of(xy_bytes(s_got.at[0], 4), recv_sem.at[9]).wait()
+    with jax.named_scope("w" + str(6)):
+        all_of(xy_bytes(e_got.at[0], 2), recv_sem.at[6]).wait()
+    with jax.named_scope("w" + str(9)):
+        all_of(xy_bytes(s_got.at[0], 4), recv_sem.at[9]).wait()
     middle(0)
-    all_of(z_bytes(e_got.at[1]), recv_sem.at[7]).wait()
-    all_of(z_bytes(s_got.at[1]), recv_sem.at[8]).wait()
+    with jax.named_scope("w" + str(7)):
+        all_of(z_bytes(e_got.at[1]), recv_sem.at[7]).wait()
+    with jax.named_scope("w" + str(8)):
+        all_of(z_bytes(s_got.at[1]), recv_sem.at[8]).wait()
     middle(1)
 
     c0, s0 = cs(1, 1, (128, 256))
@@ -259,14 +280,18 @@
                         ck * own + sk * far if part == 0 else ck * own - sk * far
                     )
 
-    all_of(xy_bytes(t_mid.at[0], 4), recv_sem.at[11]).wait()
+    with jax.named_scope("w" + str(11)):
+        all_of(xy_bytes(t_mid.at[0], 4), recv_sem.at[11]).wait()
     remote(t_mid.at[0], t_oth.at[0], 12, partner).start()
-    all_of(t_oth.at[0], recv_sem.at[12]).wait()
+    with jax.named_scope("w" + str(12)):
+        all_of(t_oth.at[0], recv_sem.at[12]).wait()
     core_mixed(0)
     send_z(t_mix.at[0], t_got.at[0], 13)
-    all_of(z_bytes(t_mid.at[1]), recv_sem.at[10]).wait()
+    with jax.named_scope("w" + str(10)):
+        all_of(z_bytes(t_mid.at[1]), recv_sem.at[10]).wait()
     remote(t_mid.at[1], t_oth.at[1], 14, partner).start()
-    all_of(t_oth.at[1], recv_sem.at[14]).wait()
+    with jax.named_scope("w" + str(14)):
+        all_of(t_oth.at[1], recv_sem.at[14]).wait()
     core_mixed(1)
     send_xy(t_mix.at[1], t_got.at[1], 15, 4)
 
@@ -287,9 +312,11 @@
                         at:at + 16, r1 * 128:r1 * 128 + 128
                     ]
 
-    all_of(xy_bytes(t_got.at[1], 4), recv_sem.at[15]).wait()
+    with jax.named_scope("w" + str(15)):
+        all_of(xy_bytes(t_got.at[1], 4), recv_sem.at[15]).wait()
     final(1)
-    all_of(z_bytes(t_got.at[0]), recv_sem.at[13]).wait()
+    with jax.named_scope("w" + str(13)):
+        all_of(z_bytes(t_got.at[0]), recv_sem.at[13]).wait()
     final(0)
 
     for there, device in xy_peers:
@@ -297,14 +324,16 @@
             p_send.at[:, pl.ds(pl.multiple_of(there * 16, 16), 16), :], p_got.at[xy], 16, device
         ).start()
     p_got[xy] = p_send[:, pl.ds(pl.multiple_of(xy * 16, 16), 16), :]
-    all_of(p_got.at[pl.ds(0, 15)], recv_sem.at[16]).wait()
+    with jax.named_scope("w" + str(16)):
+        all_of(p_got.at[pl.ds(0, 15)], recv_sem.at[16]).wait()
     total = p_got[0]
     for k in range(1, 16):
         total = total + p_got[k]
     p_sum[...] = total
     far = remote(p_sum.at[1 - z_hi], p_far, 17, ((1 - z_hi) * 16 + xy, lane))
     far.start()
-    all_of(p_far, recv_sem.at[17]).wait()
+    with jax.named_scope("w" + str(17)):
+        all_of(p_far, recv_sem.at[17]).wait()
     whole = (p_sum[z_hi] + p_far[...]) * (1.0 / 32.0)
     for t in range(4):
         marg[t] = whole[t * 4:t * 4 + 4, :]
@@ -332,9 +361,14 @@
             jax.ShapeDtypeStruct((2, 4, 128, 128), F32),
             jax.ShapeDtypeStruct((4, 4, 128), F32),
         ),
-        in_specs=[vmem] * 4,
+        in_specs=[pl.BlockSpec(memory_space=pltpu.HBM)] * 4,
         out_specs=(vmem, vmem),
         scratch_shapes=[
+            pltpu.VMEM((2, 4, 128, 128), F32),
+            pltpu.VMEM((4, 128, 128), F32),
+            pltpu.VMEM((2, 128), F32),
+            pltpu.VMEM((2, 4), F32),
+            pltpu.SemaphoreType.DMA((4,)),
             pltpu.VMEM((6, 2, 256, 256), BF16),
             pltpu.VMEM((512, 256), F32),
             wide, wide,
@@ -352,7 +386,7 @@
         compiler_params=pltpu.CompilerParams(
             collective_id=0, has_side_effects=True, vmem_limit_bytes=48 * 1024 * 1024
         ),
-    )(amplitudes, energies, phase_angles, mix_angles)
+    )(*[pltpu.with_memory_space_constraint(a, pltpu.HBM) for a in (amplitudes, energies, phase_angles, mix_angles)])
 
 
 def solution(mesh):

time: 61.8 us -> 58.6 us (0.948)
  local copies, waits for them, and re-layouts: 4.73 us -> 1.39 us
    unnamed x10 -> x2, local copies, waits for them, and re-layouts: 4.73 us -> 1.39 us
where the time goes in v2:
time: 58.6 us; the launch traced here: 58.3 us
  Pallas kernels  56.2 us (96%)
  local copies, waits for them, and re-layouts  1.39 us (2%)
  between operations  0.64 us (1%)
    pallas_call x1, Pallas kernels, on_device(): pl.pallas_call(kernel, out_shape=(jax.ShapeDtypeStruct((2, 4, 128, 128),...  56.2 us
    unnamed x2, local copies, waits for them, and re-layouts  1.39 us

profile of v2, /device:TPU:2, one launch (start us, length us, event | category | flops | bytes accessed | tf_op | source)
XLA Modules:
  0.0 58.3 jit_solution(11295432130662492709)
XLA Ops:
  0.6 56.2 %shard_map.59 = (f32[2,4,128,128]{3,2,1,0:T(8,128)S(1)}, f32[4,4,128]{2,1,0:T(4,128)S(1)}) custom-call(f32[2,4,128,128]{3,2,1,0:T(8,128)} %amps_in.1, f32[4,128,128]{2,1,0:T(8,128)} %energies_in.1, f32[2,128]{1,0:T(2,128)} %phases_in.1, f32[2,4]{1,0:T(2,128)} %mixes_in.1), custom_call_target="tpu_custom_call" | custom-call | tf_op jit(solution)/shard_map/pallas_call | solution.py:358
  56.9 0.8 %copy.8 = f32[2,4,128,128]{3,2,1,0:T(8,128)} copy(f32[2,4,128,128]{3,2,1,0:T(8,128)S(1)} %get-tuple-element.4) | data formatting | bytes 1048576
  57.7 0.6 %copy.9 = f32[4,4,128]{2,1,0:T(4,128)} copy(f32[4,4,128]{2,1,0:T(4,128)S(1)} %get-tuple-element.5) | data formatting | bytes 16384

commit v3 on v1

v3 whole, which is shorter than its diff:
```python
import functools

import jax
import jax.numpy as jnp
from jax import lax
from jax.experimental import pallas as pl
from jax.experimental.pallas import tpu as pltpu
from jax.sharding import PartitionSpec as P

MESH = pl.DeviceIdType.MESH
F32 = jnp.float32
BF16 = jnp.bfloat16

Z_STEPS = (4, 3, 5, 2, 6, 1, 7)
XY_STEPS = tuple((dx, dy) for dx in (2, 1, 3, 0) for dy in (2, 1, 3, 0) if dx or dy)
ORDER = (0, 2, 1, 3)
Z_FIRST, XY_FIRST = (0, 1), (2, 3)
STAGES = 34


def sine_cosine(angle):
    half = 0.5 * angle
    w = half * half
    s = jnp.full_like(w, -1.0 / 39916800.0)
    for term in (1.0 / 362880.0, -1.0 / 5040.0, 1.0 / 120.0, -1.0 / 6.0, 1.0):
        s = s * w + term
    s = s * half
    c = jnp.full_like(w, 1.0 / 479001600.0)
    for term in (-1.0 / 3628800.0, 1.0 / 40320.0, -1.0 / 720.0, 1.0 / 24.0, -0.5, 1.0):
        c = c * w + term
    return 2.0 * s * c, 1.0 - 2.0 * s * s


def split(value):
    high = value.astype(BF16)
    return high, (value - high.astype(F32)).astype(BF16)


def times(left, right):
    (lh, ll), (rh, rl) = left, right
    dot = functools.partial(jnp.dot, preferred_element_type=F32)
    return dot(lh, rh) + dot(lh, rl) + dot(ll, rh)


def kernel(amps_in, energies_in, phases_in, mixes_in, out, marg, *scratch):
    (amps, energies, phases, mixes, in_sem, tables, canon, moved, other, e_send, e_mid, e_got, s_buf, s_mid, s_got,
     held, held_far, t_buf, t_mid, t_got, last, p_send, p_got, p_sum, p_far, send_sem, recv_sem) = scratch
    bank, lane = lax.axis_index("bank"), lax.axis_index("lane")
    x, y, z_hi = bank % 4, (bank // 4) % 4, bank // 16
    z, core = z_hi * 4 + lane // 2, lane % 2
    xy = y * 4 + x

    def z_peer(step):
        there = (z + step) % 8
        return there, ((there // 4) * 16 + xy, (there % 4) * 2 + core)

    def xy_peer(step):
        there = ((y + step[1]) % 4) * 4 + (x + step[0]) % 4
        return there, (z_hi * 16 + there, lane)

    partner = (bank, (lane // 2) * 2 + 1 - core)
    z_peers = [z_peer(step) for step in Z_STEPS]
    xy_peers = [xy_peer(step) for step in XY_STEPS]

    barrier = pltpu.get_barrier_semaphore()
    for _, device in z_peers + xy_peers:
        pl.semaphore_signal(barrier, inc=1, device_id=device, device_id_type=MESH)
    pl.semaphore_signal(barrier, inc=1, device_id=partner, device_id_type=MESH)
    loads = [
        pltpu.make_async_copy(src, dst, in_sem.at[k])
        for k, (src, dst) in enumerate(
            ((energies_in, energies), (mixes_in, mixes), (phases_in, phases), (amps_in, amps))
        )
    ]
    for load in loads:
        load.start()

    sent = []

    def remote(src, dst, stage, device):
        return pltpu.make_async_remote_copy(
            src_ref=src, dst_ref=dst, send_sem=send_sem.at[stage], recv_sem=recv_sem.at[stage],
            device_id=device, device_id_type=MESH,
        )

    def all_of(ref, sem):
        return pltpu.make_async_copy(ref, ref, sem)

    def arrived(ref, stage):
        with jax.named_scope(f"w{stage}"):
            all_of(ref, recv_sem.at[stage]).wait()

    def send_z(src, dst, stage):
        for there, device in z_peers:
            remote(src.at[there], dst.at[z], stage, device).start()
        dst[z] = src[z]
        sent.append((src.at[pl.ds(0, 7)], stage))

    def send_xy(src, dst, stage, unit):
        own = pl.ds(xy * unit, unit)
        for there, device in xy_peers:
            remote(src.at[:, pl.ds(there * unit, unit), :], dst.at[:, own, :], stage, device).start()
        dst[:, own, :] = src[:, own, :]
        sent.append((src.at[:, pl.ds(0, 15 * unit), :], stage))

    def swap(src, dst, stage):
        remote(src, dst, stage, partner).start()
        sent.append((src, stage))

    def came_z(buf, stage):
        arrived(buf.at[pl.ds(0, 7)], stage)

    def came_xy(buf, stage, unit):
        arrived(buf.at[:, pl.ds(0, 15 * unit), :], stage)

    E1, E2, S1, S2, D1, D2, T1, T2, P1, P2 = 0, 4, 8, 12, 16, 20, 24, 28, 32, 33

    loads[0].wait()
    for q in range(4):
        for sz in range(8):
            e_send[q, sz] = energies[sz // 2, pl.ds((sz % 2) * 64 + q, 16, stride=4), :]
    with jax.named_scope("barrier"):
        pl.semaphore_wait(barrier, 23)
    for q in Z_FIRST:
        send_z(e_send.at[q], e_mid.at[q], E1 + q)
    for q in XY_FIRST:
        send_xy(e_send.at[q], e_mid.at[q], E1 + q, 1)

    for load in loads[1:]:
        load.wait()
    mix_sin, mix_cos = sine_cosine(mixes[...])

    def cs(layer, group, shape):
        at = (slice(layer, layer + 1), slice(group, group + 1))
        return jnp.broadcast_to(mix_cos[at], shape), jnp.broadcast_to(mix_sin[at], shape)

    row = lax.broadcasted_iota(jnp.int32, (128, 128), 0)
    column = lax.broadcasted_iota(jnp.int32, (128, 128), 1)
    apart = row ^ column

    def build(slot, layer, groups, on_left):
        size, count = None, None
        for k, group in enumerate(groups):
            c, s = cs(layer, group, (128, 128))
            bit = (apart >> k) & 1
            factor = jnp.where(bit == 1, s, c)
            size = factor if size is None else size * factor
            count = bit if count is None else count + bit
        odd = (count & 1) == 1
        sign = 1.0 - (count & 2).astype(F32)
        re = jnp.where(odd, 0.0, size * sign)
        im = jnp.where(odd, -size * sign, 0.0)
        for half, (real, imag) in enumerate(zip(split(re), split(im))):
            tables[slot, half, 0:128, 0:128] = real
            tables[slot, half, 128:256, 128:256] = real
            tables[slot, half, 0:128, 128:256] = -imag if on_left else imag
            tables[slot, half, 128:256, 0:128] = imag if on_left else -imag

    def table(slot):
        return tables[slot, 0], tables[slot, 1]

    lanes = (0,) * 7
    rows = (1,) * 5 + (2, 2)
    chips = (2,) * 4 + (3, 3) + (2,)
    build(0, 0, lanes, False)
    build(1, 0, rows, True)

    def turned(re, im, levels, layer):
        angle = jnp.broadcast_to(phases[layer:layer + 1, :], levels.shape) * levels
        s, c = sine_cosine(angle)
        return re * c + im * s, im * c - re * s

    def mixed(u, v, c, s):
        (ur, ui), (vr, vi) = u, v
        return (c * ur + s * vi, c * ui - s * vr), (c * vr + s * ui, c * vi - s * ur)

    c1, s1 = cs(0, 1, (32, 128))
    for t in range(4):
        parts = {}
        for q in range(4):
            at = pl.ds(q, 32, stride=4)
            parts[q] = turned(amps[0, t, at, :], amps[1, t, at, :], energies[t, at, :], 0)
        for low, high in ((0, 1), (2, 3), (0, 2), (1, 3)):
            parts[low], parts[high] = mixed(parts[low], parts[high], c1, s1)
        for q in range(4):
            for part in range(2):
                canon[q, t * 32:t * 32 + 32, part * 128:part * 128 + 128] = parts[q][part]
    for q in ORDER:
        done = times(split(canon[q]), table(0))
        moved[q, 0:128, :] = done[:, 0:128]
        moved[q, 128:256, :] = done[:, 128:256]
        swap(moved.at[q], other.at[q], D1 + q)

    def core_mixed(near, far, q, layer):
        c, s = cs(layer, 3, (128, 128))
        re = c * near[q, 0:128, :] + s * far[q, 128:256, :]
        im = c * near[q, 128:256, :] - s * far[q, 0:128, :]
        return jnp.concatenate([re, im], axis=0)

    def spread(buf, q, value):
        for sz in range(8):
            for part in range(2):
                at = part * 128 + sz * 16
                buf[q, sz, pl.ds(part, 16, stride=2), :] = value[at:at + 16, :]

    def gathered(buf, q):
        return jnp.concatenate(
            [buf[q, sz, pl.ds(part, 16, stride=2), :] for part in range(2) for sz in range(8)], axis=0
        )

    for q in ORDER:
        arrived(other.at[q], D1 + q)
        spread(s_buf, q, times(table(1), split(core_mixed(moved, other, q, 0))))
        if q in Z_FIRST:
            send_z(s_buf.at[q], s_mid.at[q], S1 + q)
        else:
            send_xy(s_buf.at[q], s_mid.at[q], S1 + q, 2)
    build(2, 0, chips, True)

    for q in XY_FIRST:
        came_xy(e_mid.at[q], E1 + q, 1)
        send_z(e_mid.at[q], e_got.at[q], E2 + q)
    for q in Z_FIRST:
        came_z(e_mid.at[q], E1 + q)
        send_xy(e_mid.at[q], e_got.at[q], E2 + q, 1)
    build(3, 1, chips, True)
    build(4, 1, lanes, False)
    build(5, 1, rows, True)

    def forward(q):
        if q in Z_FIRST:
            came_z(s_mid.at[q], S1 + q)
            send_xy(s_mid.at[q], s_got.at[q], S2 + q, 2)
        else:
            came_xy(s_mid.at[q], S1 + q, 2)
            send_z(s_mid.at[q], s_got.at[q], S2 + q)

    def middle(q):
        if q in Z_FIRST:
            came_xy(e_got.at[q], E2 + q, 1)
            came_xy(s_got.at[q], S2 + q, 2)
        else:
            came_z(e_got.at[q], E2 + q)
            came_z(s_got.at[q], S2 + q)
        value = times(table(2), split(gathered(s_got, q)))
        levels = jnp.concatenate([e_got[q, sz] for sz in range(8)], axis=0)
        value = jnp.concatenate(turned(value[0:128, :], value[128:256, :], levels, 1), axis=1)
        value = times(split(value), table(4))
        value = jnp.concatenate([value[:, 0:128], value[:, 128:256]], axis=0)
        held[q] = times(table(3), split(value))
        swap(held.at[q], held_far.at[q], D2 + q)

    def back(q):
        arrived(held_far.at[q], D2 + q)
        spread(t_buf, q, core_mixed(held, held_far, q, 1))
        if q in Z_FIRST:
            send_z(t_buf.at[q], t_mid.at[q], T1 + q)
        else:
            send_xy(t_buf.at[q], t_mid.at[q], T1 + q, 2)

    def home(q):
        if q in Z_FIRST:
            came_z(t_mid.at[q], T1 + q)
            send_xy(t_mid.at[q], t_got.at[q], T2 + q, 2)
        else:
            came_xy(t_mid.at[q], T1 + q, 2)
            send_z(t_mid.at[q], t_got.at[q], T2 + q)

    def final(q):
        if q in Z_FIRST:
            came_xy(t_got.at[q], T2 + q, 2)
        else:
            came_z(t_got.at[q], T2 + q)
        last[q] = times(table(5), split(gathered(t_got, q)))

    cr, sr = cs(1, 1, (128, 128))

    def pair(low, high):
        first, second = mixed(
            (last[low, 0:128, :], last[low, 128:256, :]), (last[high, 0:128, :], last[high, 128:256, :]), cr, sr
        )
        for q, value in ((low, first), (high, second)):
            last[q, 0:128, :], last[q, 128:256, :] = value

    forward(0)
    forward(2)
    forward(3)
    forward(1)
    middle(0)
    back(0)
    middle(1)
    middle(2)
    back(1)
    back(2)
    middle(3)
    back(3)
    home(0)
    home(2)
    home(1)
    home(3)
    final(0)
    final(2)
    pair(0, 2)
    final(1)
    final(3)
    pair(1, 3)
    pair(0, 1)
    pair(2, 3)

    for q in range(4):
        chance = last[q, 0:128, :] * last[q, 0:128, :] + last[q, 128:256, :] * last[q, 128:256, :]
        for t in range(4):
            for r6 in range(2):
                at = t * 32 + r6 * 16
                p_send[r6, pl.ds(t * 4 + q, 16, stride=16), :] = chance[at:at + 16, :]
    for there, device in xy_peers:
        remote(p_send.at[:, pl.ds(pl.multiple_of(there * 16, 16), 16), :], p_got.at[xy], P1, device).start()
    p_got[xy] = p_send[:, pl.ds(pl.multiple_of(xy * 16, 16), 16), :]
    for q in range(4):
        for part in range(2):
            for t in range(4):
                at = part * 128 + t * 32
                out[part, t, pl.ds(q, 32, stride=4), :] = last[q, at:at + 32, :]
    arrived(p_got.at[pl.ds(0, 15)], P1)
    total = p_got[0]
    for k in range(1, 16):
        total = total + p_got[k]
    p_sum[...] = total
    remote(p_sum.at[1 - z_hi], p_far, P2, ((1 - z_hi) * 16 + xy, lane)).start()
    sent.append((p_got.at[pl.ds(0, 15)], P1))
    for buf, stage in sent:
        all_of(buf, send_sem.at[stage]).wait()
    arrived(p_far, P2)
    whole = (p_sum[z_hi] + p_far[...]) * (1.0 / 32.0)
    for t in range(4):
        marg[t] = whole[t * 4:t * 4 + 4, :]
    all_of(p_far, send_sem.at[P2]).wait()


def on_device(amplitudes, energies, phase_angles, mix_angles):
    vmem = pl.BlockSpec(memory_space=pltpu.VMEM)
    state = pltpu.VMEM((4, 8, 32, 128), F32)
    levels = pltpu.VMEM((4, 8, 16, 128), F32)
    tall = pltpu.VMEM((4, 256, 128), F32)
    return pl.pallas_call(
        kernel,
        out_shape=(
            jax.ShapeDtypeStruct((2, 4, 128, 128), F32),
            jax.ShapeDtypeStruct((4, 4, 128), F32),
        ),
        in_specs=[pl.BlockSpec(memory_space=pltpu.HBM)] * 4,
        out_specs=(vmem, vmem),
        scratch_shapes=[
            pltpu.VMEM((2, 4, 128, 128), F32),
            pltpu.VMEM((4, 128, 128), F32),
            pltpu.VMEM((2, 128), F32),
            pltpu.VMEM((2, 4), F32),
            pltpu.SemaphoreType.DMA((4,)),
            pltpu.VMEM((6, 2, 256, 256), BF16),
            pltpu.VMEM((4, 128, 256), F32),
            tall, tall,
            levels, levels, levels,
            state, state, state,
            tall, tall,
            state, state, state,
            tall,
            pltpu.VMEM((2, 256, 128), F32),
            pltpu.VMEM((16, 2, 16, 128), F32),
            pltpu.VMEM((2, 16, 128), F32),
            pltpu.VMEM((16, 128), F32),
            pltpu.SemaphoreType.DMA((STAGES,)),
            pltpu.SemaphoreType.DMA((STAGES,)),
        ],
        compiler_params=pltpu.CompilerParams(
            collective_id=0, has_side_effects=True, vmem_limit_bytes=48 * 1024 * 1024
        ),
    )(*[pltpu.with_memory_space_constraint(a, pltpu.HBM) for a in (amplitudes, energies, phase_angles, mix_angles)])


def solution(mesh):
    placed = (P(None, ("bank", "lane"), None, None), P(("bank", "lane"), None, None), P(), P())
    return jax.shard_map(
        on_device,
        mesh=mesh,
        in_specs=placed,
        out_specs=(P(None, ("bank", "lane"), None, None), P("lane", "bank", None)),
        check_vma=False,
    )
```

time: 61.8 us -> 54.1 us (0.88)
  Pallas kernels: 55.9 us -> 51.9 us
  local copies, waits for them, and re-layouts: 4.73 us -> 1.39 us
    pallas_call x1, Pallas kernels: 55.9 us -> 51.9 us  [on_device(): pl.pallas_call(kernel, out_shape=(jax.ShapeDtypeStruct((2, 4, 128, 128),...]
    unnamed x10 -> x2, local copies, waits for them, and re-layouts: 4.73 us -> 1.39 us
where the time goes in v3:
time: 54.1 us; the launch traced here: 54 us
  Pallas kernels  51.9 us (96%)
  local copies, waits for them, and re-layouts  1.39 us (3%)
  between operations  0.64 us (1%)
    pallas_call x1, Pallas kernels, on_device(): pl.pallas_call(kernel, out_shape=(jax.ShapeDtypeStruct((2, 4, 128, 128),...  51.9 us
    unnamed x2, local copies, waits for them, and re-layouts  1.39 us

profile of v3, /device:TPU:2, one launch (start us, length us, event | category | flops | bytes accessed | tf_op | source)
XLA Modules:
  0.0 54.0 jit_solution(13874874140741336039)
XLA Ops:
  0.6 51.9 %shard_map.59 = (f32[2,4,128,128]{3,2,1,0:T(8,128)S(1)}, f32[4,4,128]{2,1,0:T(4,128)S(1)}) custom-call(f32[2,4,128,128]{3,2,1,0:T(8,128)} %amps_in.1, f32[4,128,128]{2,1,0:T(8,128)} %energies_in.1, f32[2,128]{1,0:T(2,128)} %phases_in.1, f32[2,4]{1,0:T(2,128)} %mixes_in.1), custom_call_target="tpu_custom_call" | custom-call | tf_op jit(solution)/shard_map/pallas_call | solution.py:345
  52.6 0.8 %copy.8 = f32[2,4,128,128]{3,2,1,0:T(8,128)} copy(f32[2,4,128,128]{3,2,1,0:T(8,128)S(1)} %get-tuple-element.4) | data formatting | bytes 1048576
  53.4 0.6 %copy.9 = f32[4,4,128]{2,1,0:T(4,128)} copy(f32[4,4,128]{2,1,0:T(4,128)S(1)} %get-tuple-element.5) | data formatting | bytes 16384

commit v4 on v3

--- a/solution.py
+++ b/solution.py
@@ -12,10 +12,10 @@
 BF16 = jnp.bfloat16
 
 Z_STEPS = (4, 3, 5, 2, 6, 1, 7)
-XY_STEPS = tuple((dx, dy) for dx in (2, 1, 3, 0) for dy in (2, 1, 3, 0) if dx or dy)
+XY_STEPS = ((2, 2), (1, 2), (3, 2), (0, 2), (2, 1), (2, 3), (1, 1), (3, 3), (0, 1), (0, 3), (1, 3), (3, 1), (2, 0), (1, 0), (3, 0))
 ORDER = (0, 2, 1, 3)
 Z_FIRST, XY_FIRST = (0, 1), (2, 3)
-STAGES = 34
+STAGES = 35
 
 
 def sine_cosine(angle):
@@ -113,7 +113,7 @@
     def came_xy(buf, stage, unit):
         arrived(buf.at[:, pl.ds(0, 15 * unit), :], stage)
 
-    E1, E2, S1, S2, D1, D2, T1, T2, P1, P2 = 0, 4, 8, 12, 16, 20, 24, 28, 32, 33
+    E1, E2, S1, S2, D1, D2, T1, T2, P1, P2 = 0, 4, 8, 12, 16, 20, 24, 28, 32, 34
 
     loads[0].wait()
     for q in range(4):
@@ -313,28 +313,44 @@
             for r6 in range(2):
                 at = t * 32 + r6 * 16
                 p_send[r6, pl.ds(t * 4 + q, 16, stride=16), :] = chance[at:at + 16, :]
-    for there, device in xy_peers:
-        remote(p_send.at[:, pl.ds(pl.multiple_of(there * 16, 16), 16), :], p_got.at[xy], P1, device).start()
-    p_got[xy] = p_send[:, pl.ds(pl.multiple_of(xy * 16, 16), 16), :]
+    for half, stage in ((1 - z_hi, P1), (z_hi, P1 + 1)):
+        for there, device in xy_peers:
+            remote(
+                p_send.at[half, pl.ds(pl.multiple_of(there * 16, 16), 16), :], p_got.at[stage - P1, xy], stage, device
+            ).start()
+        p_got[stage - P1, xy] = p_send[half, pl.ds(pl.multiple_of(xy * 16, 16), 16), :]
+        sent.append((p_got.at[stage - P1, pl.ds(0, 15)], stage))
     for q in range(4):
         for part in range(2):
             for t in range(4):
                 at = part * 128 + t * 32
                 out[part, t, pl.ds(q, 32, stride=4), :] = last[q, at:at + 32, :]
-    arrived(p_got.at[pl.ds(0, 15)], P1)
-    total = p_got[0]
-    for k in range(1, 16):
-        total = total + p_got[k]
-    p_sum[...] = total
-    remote(p_sum.at[1 - z_hi], p_far, P2, ((1 - z_hi) * 16 + xy, lane)).start()
-    sent.append((p_got.at[pl.ds(0, 15)], P1))
+
+    def summed(half):
+        arrived(p_got.at[half, pl.ds(0, 15)], P1 + half)
+        parts = [p_got[half, k] for k in range(16)]
+        while len(parts) > 1:
+            parts = [parts[k] + parts[k + 1] for k in range(0, len(parts), 2)]
+        return parts[0]
+
+    p_sum[...] = summed(0)
+    remote(p_sum, p_far, P2, ((1 - z_hi) * 16 + xy, lane)).start()
+    near = summed(1)
     for buf, stage in sent:
         all_of(buf, send_sem.at[stage]).wait()
     arrived(p_far, P2)
-    whole = (p_sum[z_hi] + p_far[...]) * (1.0 / 32.0)
+    marg[...] = (near + p_far[...]) * (1.0 / 32.0)
+    all_of(p_far, send_sem.at[P2]).wait()
+
+
+def writer(parts, chance, parts_out, chance_out, staged, sem):
+    copies = [pltpu.make_async_copy(parts, parts_out, sem.at[0]), pltpu.make_async_copy(staged, chance_out, sem.at[1])]
+    copies[0].start()
     for t in range(4):
-        marg[t] = whole[t * 4:t * 4 + 4, :]
-    all_of(p_far, send_sem.at[P2]).wait()
+        staged[t] = chance[t * 4:t * 4 + 4, :]
+    copies[1].start()
+    for copy in copies:
+        copy.wait()
 
 
 def on_device(amplitudes, energies, phase_angles, mix_angles):
@@ -342,11 +358,11 @@
     state = pltpu.VMEM((4, 8, 32, 128), F32)
     levels = pltpu.VMEM((4, 8, 16, 128), F32)
     tall = pltpu.VMEM((4, 256, 128), F32)
-    return pl.pallas_call(
+    parts, chance = pl.pallas_call(
         kernel,
         out_shape=(
             jax.ShapeDtypeStruct((2, 4, 128, 128), F32),
-            jax.ShapeDtypeStruct((4, 4, 128), F32),
+            jax.ShapeDtypeStruct((16, 128), F32),
         ),
         in_specs=[pl.BlockSpec(memory_space=pltpu.HBM)] * 4,
         out_specs=(vmem, vmem),
@@ -365,8 +381,8 @@
             state, state, state,
             tall,
             pltpu.VMEM((2, 256, 128), F32),
-            pltpu.VMEM((16, 2, 16, 128), F32),
-            pltpu.VMEM((2, 16, 128), F32),
+            pltpu.VMEM((2, 16, 16, 128), F32),
+            pltpu.VMEM((16, 128), F32),
             pltpu.VMEM((16, 128), F32),
             pltpu.SemaphoreType.DMA((STAGES,)),
             pltpu.SemaphoreType.DMA((STAGES,)),
@@ -375,6 +391,18 @@
             collective_id=0, has_side_effects=True, vmem_limit_bytes=48 * 1024 * 1024
         ),
     )(*[pltpu.with_memory_space_constraint(a, pltpu.HBM) for a in (amplitudes, energies, phase_angles, mix_angles)])
+    hbm = pl.BlockSpec(memory_space=pltpu.HBM)
+    return pl.pallas_call(
+        writer,
+        out_shape=(
+            jax.ShapeDtypeStruct((2, 4, 128, 128), F32),
+            jax.ShapeDtypeStruct((4, 4, 128), F32),
+        ),
+        in_specs=[vmem] * 2,
+        out_specs=(hbm, hbm),
+        scratch_shapes=[pltpu.VMEM((4, 4, 128), F32), pltpu.SemaphoreType.DMA((2,))],
+        compiler_params=pltpu.CompilerParams(vmem_limit_bytes=1024 * 1024),
+    )(parts, chance)
 
 
 def solution(mesh):

time: 54.1 us -> 52.9 us (0.978)
  local copies, waits for them, and re-layouts: 1.39 us -> 0 us
    unnamed x2 -> x0, local copies, waits for them, and re-layouts: 1.39 us -> none
    pallas_call x0 -> x1, Pallas kernels: none -> 0.81 us  [on_device(): pl.pallas_call(writer, out_shape=(jax.ShapeDtypeStruct((2, 4, 128, 128),...]
    pallas_call x1, Pallas kernels: 51.9 us -> 51.3 us  [on_device(): pl.pallas_call(kernel, out_shape=(jax.ShapeDtypeStruct((2, 4, 128, 128),...]
where the time goes in v4:
time: 52.9 us; the launch traced here: 52.8 us
  Pallas kernels  52.2 us (99%)
  between operations  0.64 us (1%)
    pallas_call x1, Pallas kernels, on_device(): pl.pallas_call(kernel, out_shape=(jax.ShapeDtypeStruct((2, 4, 128, 128),...  51.3 us

profile of v4, /device:TPU:2, one launch (start us, length us, event | category | flops | bytes accessed | tf_op | source)
XLA Modules:
  0.0 52.8 jit_solution(13154209394768147041)
XLA Ops:
  0.6 51.3 %shard_map.59 = (f32[2,4,128,128]{3,2,1,0:T(8,128)S(1)}, f32[16,128]{1,0:T(8,128)S(1)}) custom-call(f32[2,4,128,128]{3,2,1,0:T(8,128)} %amps_in.1, f32[4,128,128]{2,1,0:T(8,128)} %energies_in.1, f32[2,128]{1,0:T(2,128)} %phases_in.1, f32[2,4]{1,0:T(2,128)} %mixes_in.1), custom_call_target="tpu_custom_call" | custom-call | tf_op jit(solution)/shard_map/pallas_call | solution.py:361
  52.0 0.8 %shard_map.60 = (f32[2,4,128,128]{3,2,1,0:T(8,128)}, f32[4,4,128]{2,1,0:T(4,128)}) custom-call(f32[2,4,128,128]{3,2,1,0:T(8,128)S(1)} %get-tuple-element.4.parts, f32[16,128]{1,0:T(8,128)S(1)} %get-tuple-element.5.chance), custom_call_target="tpu_custom_call" | custom-call | tf_op jit(solution)/shard_map/pallas_call | solution.py:395

commit v5 on v4

--- a/solution.py
+++ b/solution.py
@@ -39,7 +39,9 @@
 def times(left, right):
     (lh, ll), (rh, rl) = left, right
     dot = functools.partial(jnp.dot, preferred_element_type=F32)
-    return dot(lh, rh) + dot(lh, rl) + dot(ll, rh)
+    columns = rh.shape[1]
+    both = dot(lh, jnp.concatenate([rh, rl], axis=1))
+    return both[:, 0:columns] + both[:, columns:] + dot(ll, rh)
 
 
 def kernel(amps_in, energies_in, phases_in, mixes_in, out, marg, *scratch):
@@ -63,7 +65,7 @@
     xy_peers = [xy_peer(step) for step in XY_STEPS]
 
     barrier = pltpu.get_barrier_semaphore()
-    for _, device in z_peers + xy_peers:
+    for _, device in xy_peers[:5] + z_peers + xy_peers[5:]:
         pl.semaphore_signal(barrier, inc=1, device_id=device, device_id_type=MESH)
     pl.semaphore_signal(barrier, inc=1, device_id=partner, device_id_type=MESH)
     loads = [
@@ -103,6 +105,20 @@
         dst[:, own, :] = src[:, own, :]
         sent.append((src.at[:, pl.ds(0, 15 * unit), :], stage))
 
+    def level_z(src, dst, q, stage):
+        pair = pl.ds(q, 2)
+        for there, device in z_peers:
+            remote(src.at[pair, there], dst.at[pair, z], stage, device).start()
+        dst[pair, z] = src[pair, z]
+        sent.append((src.at[pair, pl.ds(0, 7)], stage))
+
+    def level_xy(src, dst, q, stage):
+        pair, own = pl.ds(q, 2), pl.ds(xy, 1)
+        for there, device in xy_peers:
+            remote(src.at[pair, :, pl.ds(there, 1), :], dst.at[pair, :, own, :], stage, device).start()
+        dst[pair, :, own, :] = src[pair, :, own, :]
+        sent.append((src.at[pair, :, pl.ds(0, 15), :], stage))
+
     def swap(src, dst, stage):
         remote(src, dst, stage, partner).start()
         sent.append((src, stage))
@@ -119,15 +135,7 @@
     for q in range(4):
         for sz in range(8):
             e_send[q, sz] = energies[sz // 2, pl.ds((sz % 2) * 64 + q, 16, stride=4), :]
-    with jax.named_scope("barrier"):
-        pl.semaphore_wait(barrier, 23)
-    for q in Z_FIRST:
-        send_z(e_send.at[q], e_mid.at[q], E1 + q)
-    for q in XY_FIRST:
-        send_xy(e_send.at[q], e_mid.at[q], E1 + q, 1)
-
-    for load in loads[1:]:
-        load.wait()
+    loads[1].wait()
     mix_sin, mix_cos = sine_cosine(mixes[...])
 
     def cs(layer, group, shape):
@@ -165,6 +173,14 @@
     build(0, 0, lanes, False)
     build(1, 0, rows, True)
 
+    with jax.named_scope("barrier"):
+        pl.semaphore_wait(barrier, 23)
+    level_z(e_send, e_mid, 0, E1)
+    level_xy(e_send, e_mid, 2, E1 + 2)
+
+    for load in loads[2:]:
+        load.wait()
+
     def turned(re, im, levels, layer):
         angle = jnp.broadcast_to(phases[layer:layer + 1, :], levels.shape) * levels
         s, c = sine_cosine(angle)
@@ -217,12 +233,10 @@
             send_xy(s_buf.at[q], s_mid.at[q], S1 + q, 2)
     build(2, 0, chips, True)
 
-    for q in XY_FIRST:
-        came_xy(e_mid.at[q], E1 + q, 1)
-        send_z(e_mid.at[q], e_got.at[q], E2 + q)
-    for q in Z_FIRST:
-        came_z(e_mid.at[q], E1 + q)
-        send_xy(e_mid.at[q], e_got.at[q], E2 + q, 1)
+    arrived(e_mid.at[pl.ds(2, 2), :, pl.ds(0, 15), :], E1 + 2)
+    level_z(e_mid, e_got, 2, E2 + 2)
+    arrived(e_mid.at[pl.ds(0, 2), pl.ds(0, 7)], E1)
+    level_xy(e_mid, e_got, 0, E2)
     build(3, 1, chips, True)
     build(4, 1, lanes, False)
     build(5, 1, rows, True)
@@ -237,10 +251,12 @@
 
     def middle(q):
         if q in Z_FIRST:
-            came_xy(e_got.at[q], E2 + q, 1)
+            if q == 0:
+                arrived(e_got.at[pl.ds(0, 2), :, pl.ds(0, 15), :], E2)
             came_xy(s_got.at[q], S2 + q, 2)
         else:
-            came_z(e_got.at[q], E2 + q)
+            if q == 2:
+                arrived(e_got.at[pl.ds(2, 2), pl.ds(0, 7)], E2 + 2)
             came_z(s_got.at[q], S2 + q)
         value = times(table(2), split(gathered(s_got, q)))
         levels = jnp.concatenate([e_got[q, sz] for sz in range(8)], axis=0)

time: 52.9 us -> 52.3 us (0.989)
  Pallas kernels: 52.2 us -> 51.5 us
    pallas_call x1, Pallas kernels: 51.3 us -> 50.7 us  [on_device(): pl.pallas_call(kernel, out_shape=(jax.ShapeDtypeStruct((2, 4, 128, 128),...]
where the time goes in v5:
time: 52.3 us; the launch traced here: 52.2 us
  Pallas kernels  51.5 us (98%)
  between operations  0.64 us (1%)
    pallas_call x1, Pallas kernels, on_device(): pl.pallas_call(kernel, out_shape=(jax.ShapeDtypeStruct((2, 4, 128, 128),...  50.7 us

profile of v5, /device:TPU:2, one launch (start us, length us, event | category | flops | bytes accessed | tf_op | source)
XLA Modules:
  0.0 52.2 jit_solution(12019956725434953576)
XLA Ops:
  0.6 50.7 %shard_map.59 = (f32[2,4,128,128]{3,2,1,0:T(8,128)S(1)}, f32[16,128]{1,0:T(8,128)S(1)}) custom-call(f32[2,4,128,128]{3,2,1,0:T(8,128)} %amps_in.1, f32[4,128,128]{2,1,0:T(8,128)} %energies_in.1, f32[2,128]{1,0:T(2,128)} %phases_in.1, f32[2,4]{1,0:T(2,128)} %mixes_in.1), custom_call_target="tpu_custom_call" | custom-call | tf_op jit(solution)/shard_map/pallas_call | solution.py:377
  51.3 0.8 %shard_map.60 = (f32[2,4,128,128]{3,2,1,0:T(8,128)}, f32[4,4,128]{2,1,0:T(4,128)}) custom-call(f32[2,4,128,128]{3,2,1,0:T(8,128)S(1)} %get-tuple-element.4.parts, f32[16,128]{1,0:T(8,128)S(1)} %get-tuple-element.5.chance), custom_call_target="tpu_custom_call" | custom-call | tf_op jit(solution)/shard_map/pallas_call | solution.py:411
